TPU v7x, 32 devices: a whole 2x2x4 slice. The times are simulated.
32 devices in a mesh: groups: 2 (over x), col: 16 (over z, y, core).
Axes of the slice: x: 2, y: 2, z: 4, core: 2. Of those that a mesh axis runs over, the one named last changes fastest.
Arguments:
- left: bfloat16 [256, 64, 32], P('col', 'groups'), parts along dimension 1, may hold values from -18 to 18
- right: bfloat16 [256, 2560, 32], P('col', 'groups'), parts along dimension 1, may hold values from -18 to 18
- out_weight: bfloat16 [1024, 128], replicated, may hold values from -0.1875 to 0.1875
- out_bias: float32 [128], replicated, may hold values from -3 to 3
Outputs:
- pair_update: bfloat16 [64, 1280, 128], P('groups', 'col'), parts along dimension 0
There are 2 independent parts, one for each index of `groups`. A program takes and returns all parts, laid end to end along the dimension named above; an argument that names none is the same for every part. Nothing has to cross between parts.
All inputs are finite; a program needn't handle non-finite values.
Results may differ from a plain program's by a relative error of at most 0.004.
Values may be sent and summed in bfloat16 or wider, within the bound.
A program may use at most 64 MiB of HBM per device.

v0:
```python
import functools

import jax
import jax.numpy as jnp
from jax import lax
from jax.experimental import pallas as pl
from jax.experimental.pallas import tpu as pltpu
from jax.sharding import PartitionSpec as P

MESH = pl.DeviceIdType.MESH
LANES = 128
TILE = 16
GROUP = 4


def flip(x_ref, o_ref, h):
    chunks, columns, lanes = o_ref.shape
    part = x_ref.shape[1] // chunks
    step = 2 * LANES
    for start in range(0, columns, step):
        piece = x_ref[:, h * part : (h + 1) * part, start : start + step]
        o_ref[h, start : start + step] = piece.reshape(lanes, step).T


def swap_matrix(first, minor, start, rows, columns):
    row = lax.broadcasted_iota(jnp.int32, (rows, columns), 0) + start
    column = lax.broadcasted_iota(jnp.int32, (rows, columns), 1)
    shift = first.bit_length() - 1
    wanted = (row & (first - 1)) * minor + (row >> shift)
    return jnp.where(column == wanted, 1.0, 0.0).astype(jnp.bfloat16)


def kernel(
    n, width, cols, rows, chunks, given_ref, left_ref, weight_ref, bias_ref, out_ref,
    right_ref, rbuf, lbuf, rwide, lturn, wturn, flat, partial,
    rsend, rrecv, lsend, lrecv, fsend, own,
):
    me = lax.axis_index("col")
    place = lax.rem(me, GROUP)
    mates = [me - place + lax.rem(place + j, GROUP) for j in range(1, GROUP)]
    hops = n // GROUP
    local = left_ref.shape[0]
    seqs = n * local
    part = width // chunks

    def rcopy(h, k):
        to = lax.rem(me + k, n)
        start = pl.multiple_of(to * cols, TILE)
        return pltpu.make_async_remote_copy(
            src_ref=right_ref.at[h, pl.ds(start, cols)],
            dst_ref=rbuf.at[h, me],
            send_sem=rsend.at[h, k],
            recv_sem=rrecv.at[h, me],
            device_id={"col": to},
            device_id_type=MESH,
        )

    def lcopy(src, slot, to, send):
        return pltpu.make_async_remote_copy(
            src_ref=src,
            dst_ref=lbuf.at[slot],
            send_sem=send,
            recv_sem=lrecv.at[slot],
            device_id={"col": to},
            device_id_type=MESH,
        )

    barrier = pltpu.get_barrier_semaphore()
    for k in range(1, n):
        pl.semaphore_signal(
            barrier, inc=1, device_id={"col": lax.rem(me + k, n)}, device_id_type=MESH
        )
    flip(given_ref, right_ref, 0)
    pl.semaphore_wait(barrier, n - 1)

    sends = []
    for k in range(1, hops):
        sends.append(lcopy(left_ref, me, lax.rem(me + GROUP * k, n), lsend.at[k]))
    for j, mate in enumerate(mates):
        sends.append(lcopy(left_ref, me, mate, fsend.at[0, j]))
    for k in range(1, n):
        sends.append(rcopy(0, k))
    for copy in sends:
        copy.start()
    for h in range(1, chunks):
        flip(given_ref, right_ref, h)
    mine_left = pltpu.make_async_copy(left_ref, lbuf.at[me], own.at[chunks])
    mine_left.start()

    rwide[...] = jnp.zeros_like(rwide)
    channels = width * width
    for start in range(0, channels, LANES):
        chosen = swap_matrix(width, width, start, LANES, channels)
        block = jnp.dot(chosen, weight_ref[...], preferred_element_type=jnp.float32)
        wturn[:, start : start + LANES] = block.T.astype(jnp.bfloat16)
    for h in range(1, chunks):
        later = [rcopy(h, k) for k in range(1, n)]
        for copy in later:
            copy.start()
        sends += later
    mine = []
    for h in range(chunks):
        block = right_ref.at[h, pl.ds(pl.multiple_of(me * cols, TILE), cols)]
        mine.append(pltpu.make_async_copy(block, rbuf.at[h, me], own.at[h]))
        mine[h].start()
    swap = swap_matrix(TILE, part, 0, TILE * part, TILE * part)

    forwards = []
    for k in range(1, hops):
        slot = lax.rem(me + n - GROUP * k, n)
        lcopy(left_ref, slot, mates[0], lsend.at[k]).wait_recv()
        for j, mate in enumerate(mates):
            forward = lcopy(lbuf.at[slot], slot, mate, fsend.at[k, j])
            forward.start()
            forwards.append(forward)
    for k in range(hops):
        for j, mate in enumerate(mates):
            slot = lax.rem(mate + n - GROUP * k, n)
            lcopy(left_ref, slot, mate, fsend.at[k, j]).wait_recv()
    mine_left.wait()
    per = TILE // local
    blocks = []
    for group in range(seqs // TILE):
        parts = [lbuf[group * per + p] for p in range(per)]
        if per > 1:
            parts = [piece.astype(jnp.float32) for piece in parts]
            blocks.append(jnp.concatenate(parts, axis=0).astype(jnp.bfloat16))
        else:
            blocks.append(parts[0])
    lturn[...] = jnp.concatenate(blocks, axis=0).T

    def turn(h, start, block):
        turned = lax.dot_general(
            swap, block, (((1,), (1,)), ((), ())), preferred_element_type=jnp.float32
        ).astype(jnp.bfloat16)
        for e in range(part):
            at = (h * part + e) * LANES
            rwide[pl.ds(start, TILE), at : at + cols] = turned[e * TILE : (e + 1) * TILE]

    def arrive(h):
        def one(k, carry):
            slot = lax.rem(me + n - k, n)
            pltpu.make_async_remote_copy(
                src_ref=right_ref.at[h, pl.ds(0, cols)],
                dst_ref=rbuf.at[h, slot],
                send_sem=rsend.at[h, k],
                recv_sem=rrecv.at[h, slot],
                device_id={"col": slot},
                device_id_type=MESH,
            ).wait_recv()
            if per == 1:
                turn(h, pl.multiple_of(slot * TILE, TILE), rbuf[h, slot])
            return carry

        mine[h].wait()
        if per == 1:
            turn(h, pl.multiple_of(me * TILE, TILE), rbuf[h, me])
        lax.fori_loop(1, n, one, 0)
        if per > 1:
            for group in range(seqs // TILE):
                parts = [rbuf[h, group * per + p] for p in range(per)]
                turn(h, group * TILE, jnp.concatenate(parts, axis=1))

    count = flat.shape[0] * 2

    def multiply(base, h):
        def outer(step, carry):
            lanes = pl.ds(pl.multiple_of(step * 2 * LANES, 2 * LANES), 2 * LANES)
            product = jnp.dot(
                lturn[base * width : (base + count) * width, :],
                rwide[:, lanes],
                preferred_element_type=jnp.float32,
            ).astype(jnp.bfloat16)
            for side_e in range(2):
                at = pl.ds(pl.multiple_of((step * 2 + side_e) * width, width), width)
                for i in range(count):
                    side = (i % 2) * LANES
                    flat[i // 2, at, side : side + LANES] = product[
                        i * width : (i + 1) * width, side_e * LANES : (side_e + 1) * LANES
                    ]
            return carry

        lax.fori_loop(h * part // 2, (h + 1) * part // 2, outer, 0)

    deep = part * width
    early = rows == count and chunks > 1

    def project_early(step, carry):
        partial[step] = jnp.dot(
            wturn[:, : channels - deep],
            flat[step, : channels - deep],
            preferred_element_type=jnp.float32,
        )
        return carry

    for h in range(chunks):
        arrive(h)
        if rows == count:
            multiply(0, h)
        if early and h == chunks - 2:
            lax.fori_loop(0, count // 2, project_early, 0)

    skip = channels - deep if early else 0
    for base in range(0, rows, count):
        if rows != count:
            for h in range(chunks):
                multiply(base, h)

        def project(step, carry):
            update = jnp.dot(
                wturn[:, skip:], flat[step, skip:], preferred_element_type=jnp.float32
            )
            if early:
                update = update + partial[step]
            update = update.T * (1.0 / seqs) + bias_ref[...]
            update = update.astype(out_ref.dtype)
            out_ref[base + 2 * step] = update[:cols]
            out_ref[base + 2 * step + 1] = update[LANES : LANES + cols]
            return carry

        lax.fori_loop(0, count // 2, project, 0)

    for copy in sends + forwards:
        copy.wait_send()


def on_device(n, left, right, out_weight, out_bias):
    local, rows, width = left.shape
    cols = right.shape[1] // n
    pair = out_weight.shape[1]
    seqs = local * n
    chunks = 2 if local * width % (4 * LANES) == 0 else 1
    rows_step = min(rows, 32)
    vmem = pl.BlockSpec(memory_space=pltpu.VMEM)
    dma = pltpu.SemaphoreType.DMA
    return pl.pallas_call(
        functools.partial(kernel, n, width, cols, rows, chunks),
        out_shape=jax.ShapeDtypeStruct((rows, cols, pair), jnp.bfloat16),
        in_specs=[vmem] * 4,
        out_specs=vmem,
        scratch_shapes=[
            pltpu.VMEM((chunks, right.shape[1], local * width // chunks), jnp.bfloat16),
            pltpu.VMEM((chunks, n, cols, local * width // chunks), jnp.bfloat16),
            pltpu.VMEM((n, local, rows * width), jnp.bfloat16),
            pltpu.VMEM((seqs, width * LANES), jnp.bfloat16),
            pltpu.VMEM((rows * width, seqs), jnp.bfloat16),
            pltpu.VMEM((pair, width * width), jnp.bfloat16),
            pltpu.VMEM((rows_step // 2, width * width, 2 * LANES), jnp.bfloat16),
            pltpu.VMEM((rows_step // 2, pair, 2 * LANES), jnp.float32),
            dma((chunks, n)), dma((chunks, n)),
            dma((n // GROUP,)), dma((n,)), dma((n // GROUP, GROUP)), dma((chunks + 1,)),
        ],
        compiler_params=pltpu.CompilerParams(
            collective_id=0, has_side_effects=True, vmem_limit_bytes=60 * 1024 * 1024
        ),
    )(jnp.transpose(right, (0, 2, 1)), left.reshape(local, rows * width), out_weight, out_bias.reshape(1, pair))


def solution(mesh):
    return jax.shard_map(
        functools.partial(on_device, mesh.shape["col"]),
        mesh=mesh,
        in_specs=(P("col", "groups", None), P("col", "groups", None), P(), P()),
        out_specs=P("groups", "col", None),
        check_vma=False,
    )
```

profile of v0, /device:TPU:29, one launch (start us, length us, event | category | flops | bytes accessed | tf_op | source)
XLA Modules:
  0.0 52.4 jit_solution(10184115690670508297)
XLA Ops:
  0.0 1.7 %reshape.6.left_ref = bf16[16,1024]{1,0:T(8,128)(2,1)} reshape(bf16[16,32,32]{2,1,0:T(8,128)(2,1)} %param.4) | data formatting | bytes 65536 | tf_op jit(solution)/shard_map/reshape | solution.py:256
  1.7 48.7 %shard_map.46 = bf16[32,80,128]{2,1,0:T(8,128)(2,1)} custom-call(bf16[16,32,1280]{2,1,0:T(8,128)(2,1)} %bitcast.2, bf16[16,1024]{1,0:T(8,128)(2,1)} %reshape.6.left_ref, bf16[1024,128]{1,0:T(8,128)(2,1)} %weight_ref.1, f32[1,128]{1,0:T(1,128)} %bitcast.3), custom_call_target="tpu_custom_call" | custom-call | tf_op jit(solution)/shard_map/pallas_call | solution.py:236
  50.4 2.0 %copy.6 = bf16[32,80,128]{2,1,0:T(8,128)(2,1)} copy(bf16[32,80,128]{2,1,0:T(8,128)(2,1)} %shard_map.46) | data formatting | bytes 1310720
where the time goes:
time: 52.6 us; the launch traced here: 52.4 us
  Pallas kernels  48.7 us (93%)
  local copies, waits for them, and re-layouts  3.66 us (7%)
    pallas_call x1, Pallas kernels, on_device(): pl.pallas_call(functools.partial(kernel, n, width, cols, rows, chunks), o...  48.7 us
    unnamed x1, local copies, waits for them, and re-layouts  1.97 us
    reshape x1, local copies, waits for them, and re-layouts, on_device(): left.reshape(local, rows * width)  1.69 us

commit v1 on v0

--- a/solution.py
+++ b/solution.py
@@ -1,4 +1,5 @@
 import functools
+import math
 
 import jax
 import jax.numpy as jnp
@@ -11,6 +12,322 @@
 LANES = 128
 TILE = 16
 GROUP = 4
+
+
+def lane_index():
+    return lax.broadcasted_iota(jnp.int32, (TILE, LANES), 1)
+
+
+def turn_lanes(x, shift):
+    shift %= LANES
+    return pltpu.roll(x, shift, axis=1) if shift else x
+
+
+def pick(lane, start, left, right):
+    return jnp.where(lane >= start, right, left)
+
+
+def pack_columns(cols, period, tiles):
+    lane = lane_index()
+    packed = []
+    for d in range(period):
+        first, offset = divmod(cols * d, LANES)
+        moved = []
+        for e in range(period):
+            piece = tiles[e][first]
+            if offset + cols > LANES:
+                piece = pick(lane, offset, tiles[e][first + 1], piece)
+            moved.append(turn_lanes(piece, cols * e - offset))
+        outs = []
+        for u in range(cols * period // LANES):
+            low, high = u * LANES, (u + 1) * LANES
+            out = None
+            for e in range(period):
+                start = cols * e
+                if start + cols <= low or start >= high:
+                    continue
+                out = moved[e] if out is None else pick(lane, start - low, out, moved[e])
+            outs.append(out)
+        packed.append(outs)
+    return packed
+
+
+def unpack_columns(cols, period, tiles):
+    lane = lane_index()
+    wide = []
+    for e in range(period):
+        first, offset = divmod(cols * e, LANES)
+        piece = tiles[first]
+        if offset + cols > LANES:
+            piece = pick(lane, offset, tiles[first + 1], piece)
+        wide.append(turn_lanes(piece, -offset))
+    return wide
+
+
+def packed_kernel(
+    n, cols, period, left_hbm, right_hbm, weight_hbm, bias_hbm, out_ref,
+    left_ref, right_ref, weight_ref, bias_ref, lspread, rspread, sbuf, rbuf, lbuf,
+    rwide, lturn, wturn, flat, partial,
+    rsend, rrecv, lsend, lrecv, loads,
+):
+    me = lax.axis_index("col")
+    half = n // 2
+    base = me // half * half
+    partner = me + 1 - 2 * lax.rem(me, 2)
+    mirror = lax.rem(me + half, n)
+    local, rows, width = left_ref.shape
+    seqs = n * local
+    chunks = width // period
+    halves = width // TILE
+    per_half = chunks // halves
+    channels = width * width
+    deep = period * width
+
+    barrier = pltpu.get_barrier_semaphore()
+    for k in range(1, n):
+        pl.semaphore_signal(
+            barrier, inc=1, device_id={"col": lax.rem(me + k, n)}, device_id_type=MESH
+        )
+    fetch_left = pltpu.make_async_copy(left_hbm, left_ref, loads.at[0])
+    fetch_weight = pltpu.make_async_copy(weight_hbm, weight_ref, loads.at[1])
+    fetch_bias = pltpu.make_async_copy(bias_hbm, bias_ref, loads.at[2])
+    fetch_right = [
+        pltpu.make_async_copy(
+            right_hbm.at[:, pl.ds(h * TILE, TILE)],
+            right_ref.at[:, pl.ds(h * TILE, TILE)],
+            loads.at[3 + h],
+        )
+        for h in range(halves)
+    ]
+    fetch_left.start()
+    for fetch in fetch_right:
+        fetch.start()
+    fetch_weight.start()
+    fetch_bias.start()
+
+    fetch_left.wait()
+    for s in range(local):
+        lspread[s * rows : (s + 1) * rows, :width] = left_ref[s].astype(jnp.float32)
+    lane = lane_index()
+    join = LANES // width
+    for t in range(rows // join):
+        block = lspread[pl.ds(t * join, local, stride=rows), :]
+        for k in range(1, join):
+            piece = lspread[pl.ds(t * join + k, local, stride=rows), :]
+            block = pick(lane, k * width, block, turn_lanes(piece, k * width))
+        lbuf[me, :, t * LANES : (t + 1) * LANES] = block.astype(jnp.bfloat16)
+
+    turns = cols * period // LANES
+    cycles = n // period
+    for h in range(halves):
+        fetch_right[h].wait()
+        for s in range(local):
+            for t in range(turns * cycles):
+                rspread[t, s * TILE : (s + 1) * TILE] = right_ref[
+                    s, h * TILE : (h + 1) * TILE, t * LANES : (t + 1) * LANES
+                ].astype(jnp.float32)
+
+        def pack(step, carry, h=h):
+            chunk, cycle = step // cycles, lax.rem(step, cycles)
+            tiles = [
+                [
+                    rspread[
+                        cycle * turns + t,
+                        pl.ds(chunk * period + e, local, stride=TILE),
+                    ].astype(jnp.bfloat16)
+                    for t in range(turns)
+                ]
+                for e in range(period)
+            ]
+            for d, outs in enumerate(pack_columns(cols, period, tiles)):
+                for u, out in enumerate(outs):
+                    sbuf[
+                        h * per_half + chunk, cycle * period + d, :,
+                        u * LANES : (u + 1) * LANES,
+                    ] = out
+            return carry
+
+        lax.fori_loop(0, per_half * cycles, pack, 0)
+
+    def rcopy(chunk, to, slot):
+        return pltpu.make_async_remote_copy(
+            src_ref=sbuf.at[chunk, to],
+            dst_ref=rbuf.at[chunk, slot],
+            send_sem=rsend.at[chunk, to],
+            recv_sem=rrecv.at[chunk, slot],
+            device_id={"col": to},
+            device_id_type=MESH,
+        )
+
+    def lcopy(slot, to, send):
+        return pltpu.make_async_remote_copy(
+            src_ref=lbuf.at[slot],
+            dst_ref=lbuf.at[slot],
+            send_sem=lsend.at[send],
+            recv_sem=lrecv.at[slot],
+            device_id={"col": to},
+            device_id_type=MESH,
+        )
+
+    pl.semaphore_wait(barrier, n - 1)
+
+    mates = [base + lax.rem(me - base + 2 * j, half) for j in range(1, half // 2)]
+    sources = [base + lax.rem(me - base + half - 2 * j, half) for j in range(1, half // 2)]
+    sends = []
+
+    def send_left(slot, to):
+        copy = lcopy(slot, to, len(sends))
+        copy.start()
+        sends.append(copy)
+
+    def other(slot):
+        return lax.rem(slot + half, n)
+
+    for to in [mirror] + mates + [partner]:
+        send_left(me, to)
+    for chunk in range(chunks):
+
+        def send_right(k, carry, chunk=chunk):
+            to = lax.rem(me + k, n)
+            rcopy(chunk, to, me).start()
+            return carry
+
+        lax.fori_loop(1, n, send_right, 0)
+
+    fetch_weight.wait()
+    fetch_bias.wait()
+    for start in range(0, channels, LANES):
+        chosen = swap_matrix(width, width, start, LANES, channels)
+        block = jnp.dot(chosen, weight_ref[...], preferred_element_type=jnp.float32)
+        wturn[:, start : start + LANES] = block.T.astype(jnp.bfloat16)
+
+    lcopy(mirror, me, 0).wait_recv()
+    for to in mates + [partner]:
+        send_left(mirror, to)
+    for source in sources:
+        for slot in (source, other(source)):
+            lcopy(slot, me, 0).wait_recv()
+            send_left(slot, partner)
+    for j in range(half // 2):
+        slot = base + lax.rem(partner - base + 2 * j, half)
+        for slot in (slot, other(slot)):
+            lcopy(slot, me, 0).wait_recv()
+    for s in range(0, n, LANES // TILE):
+        block = jnp.concatenate([lbuf[s + p] for p in range(LANES // TILE)], axis=0)
+        lturn[:, s * TILE : s * TILE + LANES] = block.T
+
+    def place(slot, block):
+        start = pl.multiple_of(slot * TILE, TILE)
+        for e, wide in enumerate(unpack_columns(cols, period, block)):
+            rwide[pl.ds(start, TILE), e * LANES : (e + 1) * LANES] = wide
+
+    def multiply(step, carry):
+        lanes = pl.ds(pl.multiple_of(step * 2 * LANES, 2 * LANES), 2 * LANES)
+        product = jnp.dot(
+            lturn[...], rwide[:, lanes], preferred_element_type=jnp.float32
+        ).astype(jnp.bfloat16)
+        for side_e in range(2):
+            at = pl.ds(pl.multiple_of((step * 2 + side_e) * width, width), width)
+            for i in range(rows):
+                side = (i % 2) * LANES
+                flat[i // 2, at, side : side + LANES] = product[
+                    i * width : (i + 1) * width, side_e * LANES : (side_e + 1) * LANES
+                ]
+        return carry
+
+    for chunk in range(chunks):
+        place(me, [sbuf[chunk, me, :, u * LANES : (u + 1) * LANES] for u in range(turns)])
+
+        def arrive(k, carry, chunk=chunk):
+            slot = lax.rem(me + n - k, n)
+            rcopy(chunk, slot, slot).wait_recv()
+            place(slot, [rbuf[chunk, slot, :, u * LANES : (u + 1) * LANES] for u in range(turns)])
+            return carry
+
+        lax.fori_loop(1, n, arrive, 0)
+        lax.fori_loop(0, period // 2, multiply, 0)
+
+        def project(pair, carry, chunk=chunk):
+            for step in (2 * pair, 2 * pair + 1):
+                update = jnp.dot(
+                    wturn[:, chunk * deep : (chunk + 1) * deep], flat[step],
+                    preferred_element_type=jnp.float32,
+                )
+                if chunk:
+                    update = update + partial[step]
+                if chunk < chunks - 1:
+                    partial[step] = update
+                else:
+                    update = update.T * (1.0 / seqs) + bias_ref[...]
+                    update = update.astype(out_ref.dtype)
+                    out_ref[2 * step] = update[:cols]
+                    out_ref[2 * step + 1] = update[LANES : LANES + cols]
+            return carry
+
+        lax.fori_loop(0, rows // 4, project, 0)
+
+    for chunk in range(chunks):
+
+        def sent(k, carry, chunk=chunk):
+            rcopy(chunk, lax.rem(me + k, n), me).wait_send()
+            return carry
+
+        lax.fori_loop(1, n, sent, 0)
+    for copy in sends:
+        copy.wait_send()
+
+
+def packed_call(n, left, right, out_weight, out_bias):
+    local, rows, width = left.shape
+    cols = right.shape[1] // n
+    pair = out_weight.shape[1]
+    seqs = local * n
+    period = LANES // math.gcd(cols, LANES)
+    chunks = width // period
+    lanes = cols * period
+    hbm = pl.BlockSpec(memory_space=pltpu.HBM)
+    vmem = pl.BlockSpec(memory_space=pltpu.VMEM)
+    dma = pltpu.SemaphoreType.DMA
+    bf16, f32 = jnp.bfloat16, jnp.float32
+    return pl.pallas_call(
+        functools.partial(packed_kernel, n, cols, period),
+        out_shape=jax.ShapeDtypeStruct((rows, cols, pair), bf16),
+        in_specs=[hbm] * 4,
+        out_specs=vmem,
+        scratch_shapes=[
+            pltpu.VMEM((local, rows, width), bf16),
+            pltpu.VMEM((local, width, n * cols), bf16),
+            pltpu.VMEM((width * width, pair), bf16),
+            pltpu.VMEM((1, pair), f32),
+            pltpu.VMEM((local * rows, LANES), f32),
+            pltpu.VMEM((n * cols // LANES, local * TILE, LANES), f32),
+            pltpu.VMEM((chunks, n, local, lanes), bf16),
+            pltpu.VMEM((chunks, n, local, lanes), bf16),
+            pltpu.VMEM((n, local, rows * width), bf16),
+            pltpu.VMEM((seqs, period * LANES), bf16),
+            pltpu.VMEM((rows * width, seqs), bf16),
+            pltpu.VMEM((pair, width * width), bf16),
+            pltpu.VMEM((rows // 2, period * width, 2 * LANES), bf16),
+            pltpu.VMEM((rows // 2, pair, 2 * LANES), f32),
+            dma((chunks, n)), dma((chunks, n)), dma((n,)), dma((n,)),
+            dma((3 + width // TILE,)),
+        ],
+        compiler_params=pltpu.CompilerParams(
+            collective_id=0, has_side_effects=True, vmem_limit_bytes=28 * 1024 * 1024
+        ),
+    )(left, jnp.transpose(right, (0, 2, 1)), out_weight, out_bias.reshape(1, pair))
+
+
+def packs(n, left, right):
+    local, rows, width = left.shape
+    cols = right.shape[1] // n
+    period = LANES // math.gcd(cols, LANES)
+    return (
+        local == TILE and cols <= LANES and rows % 4 == 0 and rows <= 32
+        and LANES % width == 0 and rows % (LANES // width) == 0
+        and width % TILE == 0 and TILE % period == 0 and period % 2 == 0
+        and n % period == 0 and n % (LANES // TILE) == 0 and n % 4 == 0
+    )
 
 
 def flip(x_ref, o_ref, h):
@@ -225,6 +542,8 @@
 
 
 def on_device(n, left, right, out_weight, out_bias):
+    if packs(n, left, right):
+        return packed_call(n, left, right, out_weight, out_bias)
     local, rows, width = left.shape
     cols = right.shape[1] // n
     pair = out_weight.shape[1]

time: 52.6 us -> 56.7 us (1.078)
  the two profiles are of different devices: /device:TPU:29 before, /device:TPU:13 now
where the time goes in v1:
time: 56.7 us; the launch traced here: 56.5 us
  Pallas kernels  51.8 us (91%)
  local copies, waits for them, and re-layouts  4.66 us (8%)
    pallas_call x1, Pallas kernels, packed_call(): pl.pallas_call(functools.partial(packed_kernel, n, cols, period), out_sha...  51.8 us
    unnamed x9, local copies, waits for them, and re-layouts  4.66 us

profile of v1, /device:TPU:13, one launch (start us, length us, event | category | flops | bytes accessed | tf_op | source)
XLA Modules:
  0.0 56.5 jit_solution(14792818668180327333)
XLA Ops:
  0.0 0.0 copy-start
  0.0 1.3 %copy-done = bf16[16,1280,32]{1,2,0:T(8,128)(2,1)S(1)} copy-done((bf16[16,1280,32]{1,2,0:T(8,128)(2,1)S(1)}, bf16[16,1280,32]{1,2,0:T(8,128)(2,1)}, u32[]{:S(2)}) %copy-start) | copy-done | bytes 1310744
  1.3 0.0 copy-start.1
  1.3 0.9 %copy-done.1 = bf16[1024,128]{1,0:T(8,128)(2,1)S(1)} copy-done((bf16[1024,128]{1,0:T(8,128)(2,1)S(1)}, bf16[1024,128]{1,0:T(8,128)(2,1)}, u32[]{:S(2)}) %copy-start.1) | copy-done | bytes 262168
  2.3 0.0 copy-start.2
  2.3 0.9 %copy-done.2 = bf16[16,32,32]{2,1,0:T(8,128)(2,1)S(1)} copy-done((bf16[16,32,32]{2,1,0:T(8,128)(2,1)S(1)}, bf16[16,32,32]{2,1,0:T(8,128)(2,1)}, u32[]{:S(2)}) %copy-start.2) | copy-done | bytes 32792
  3.2 0.0 copy-start.3
  3.2 0.7 %copy-done.3 = f32[128]{0:T(128)S(1)} copy-done((f32[128]{0:T(128)S(1)}, f32[128]{0:T(128)}, u32[]{:S(2)}) %copy-start.3) | copy-done | bytes 536
  3.8 51.8 %shard_map.46 = bf16[32,80,128]{2,1,0:T(8,128)(2,1)S(1)} custom-call(bf16[16,32,32]{2,1,0:T(8,128)(2,1)S(1)} %copy-done.2, bf16[16,32,1280]{2,1,0:T(8,128)(2,1)S(1)} %bitcast.2, bf16[1024,128]{1,0:T(8,128)(2,1)S(1)} %copy-done.1, f32[1,128]{1,0:T(1,128)S(1)} %bitcast.3), custom_call_target="tpu_custom_call" | custom-call | tf_op jit(solution)/shard_map/pallas_call | solution.py:292
  55.7 0.8 %copy.6 = bf16[32,80,128]{2,1,0:T(8,128)(2,1)} copy(bf16[32,80,128]{2,1,0:T(8,128)(2,1)S(1)} %shard_map.46) | data formatting | bytes 1310720
Async XLA Ops:
  0.0 1.3 %copy-start = (bf16[16,1280,32]{1,2,0:T(8,128)(2,1)S(1)}, bf16[16,1280,32]{1,2,0:T(8,128)(2,1)}, u32[]{:S(2)}) copy-start(bf16[16,1280,32]{1,2,0:T(8,128)(2,1)} %param.5) | copy-start | bytes 3932164
  1.3 0.9 %copy-start.1 = (bf16[1024,128]{1,0:T(8,128)(2,1)S(1)}, bf16[1024,128]{1,0:T(8,128)(2,1)}, u32[]{:S(2)}) copy-start(bf16[1024,128]{1,0:T(8,128)(2,1)} %weight_hbm.1) | copy-start | bytes 786436
  2.3 0.9 %copy-start.2 = (bf16[16,32,32]{2,1,0:T(8,128)(2,1)S(1)}, bf16[16,32,32]{2,1,0:T(8,128)(2,1)}, u32[]{:S(2)}) copy-start(bf16[16,32,32]{2,1,0:T(8,128)(2,1)} %left_hbm.1) | copy-start | bytes 98308
  3.2 0.7 %copy-start.3 = (f32[128]{0:T(128)S(1)}, f32[128]{0:T(128)}, u32[]{:S(2)}) copy-start(f32[128]{0:T(128)} %param.7) | copy-start | bytes 1540

commit v2 on v1

--- a/solution.py
+++ b/solution.py
@@ -185,15 +185,16 @@
 
     for to in [mirror] + mates + [partner]:
         send_left(me, to)
-    for chunk in range(chunks):
-
-        def send_right(k, carry, chunk=chunk):
+
+    def send_chunk(chunk):
+        def send_right(k, carry):
             to = lax.rem(me + k, n)
             rcopy(chunk, to, me).start()
             return carry
 
         lax.fori_loop(1, n, send_right, 0)
 
+    send_chunk(0)
     fetch_weight.wait()
     fetch_bias.wait()
     for start in range(0, channels, LANES):
@@ -204,6 +205,8 @@
     lcopy(mirror, me, 0).wait_recv()
     for to in mates + [partner]:
         send_left(mirror, to)
+    for chunk in range(1, chunks):
+        send_chunk(chunk)
     for source in sources:
         for slot in (source, other(source)):
             lcopy(slot, me, 0).wait_recv()
@@ -313,7 +316,7 @@
             dma((3 + width // TILE,)),
         ],
         compiler_params=pltpu.CompilerParams(
-            collective_id=0, has_side_effects=True, vmem_limit_bytes=28 * 1024 * 1024
+            collective_id=0, has_side_effects=True, vmem_limit_bytes=60 * 1024 * 1024
         ),
     )(left, jnp.transpose(right, (0, 2, 1)), out_weight, out_bias.reshape(1, pair))
 

time: 56.7 us -> 45.2 us (0.80)
  the two profiles are of different devices: /device:TPU:13 before, /device:TPU:10 now
where the time goes in v2:
time: 45.2 us; the launch traced here: 44.6 us
  Pallas kernels  42.7 us (94%)
  local copies, waits for them, and re-layouts  1.97 us (4%)
    pallas_call x1, Pallas kernels, packed_call(): pl.pallas_call(functools.partial(packed_kernel, n, cols, period), out_sha...  42.7 us
    unnamed x1, local copies, waits for them, and re-layouts  1.97 us

profile of v2, /device:TPU:10, one launch (start us, length us, event | category | flops | bytes accessed | tf_op | source)
XLA Modules:
  0.0 44.6 jit_solution(14922347289495524364)
XLA Ops:
  0.0 42.7 %shard_map.46 = bf16[32,80,128]{2,1,0:T(8,128)(2,1)} custom-call(bf16[16,32,32]{2,1,0:T(8,128)(2,1)} %left_hbm.1, bf16[16,32,1280]{2,1,0:T(8,128)(2,1)} %bitcast.2, bf16[1024,128]{1,0:T(8,128)(2,1)} %weight_hbm.1, f32[1,128]{1,0:T(1,128)} %bitcast.3), custom_call_target="tpu_custom_call" | custom-call | tf_op jit(solution)/shard_map/pallas_call | solution.py:295
  42.7 2.0 %copy.6 = bf16[32,80,128]{2,1,0:T(8,128)(2,1)} copy(bf16[32,80,128]{2,1,0:T(8,128)(2,1)} %shard_map.46) | data formatting | bytes 1310720

commit v3 on v2

--- a/solution.py
+++ b/solution.py
@@ -12,6 +12,7 @@
 LANES = 128
 TILE = 16
 GROUP = 4
+LAYERS = 4
 
 
 def lane_index():
@@ -71,10 +72,15 @@
     rsend, rrecv, lsend, lrecv, loads,
 ):
     me = lax.axis_index("col")
-    half = n // 2
+    half, span = n // 2, n // LAYERS
     base = me // half * half
+    layer = me // span
     partner = me + 1 - 2 * lax.rem(me, 2)
-    mirror = lax.rem(me + half, n)
+
+    def other(slot):
+        return (LAYERS - 1 - slot // span) * span + lax.rem(slot, span)
+
+    mirror = other(me)
     local, rows, width = left_ref.shape
     seqs = n * local
     chunks = width // period
@@ -153,22 +159,35 @@
         return pltpu.make_async_remote_copy(
             src_ref=sbuf.at[chunk, to],
             dst_ref=rbuf.at[chunk, slot],
-            send_sem=rsend.at[chunk, to],
-            recv_sem=rrecv.at[chunk, slot],
+            send_sem=rsend,
+            recv_sem=rrecv.at[chunk, slot // span],
             device_id={"col": to},
             device_id_type=MESH,
         )
 
-    def lcopy(slot, to, send):
+    def arrival(chunk, source, count):
+        slots = pl.ds(source * span, count)
+        return pltpu.make_async_remote_copy(
+            src_ref=sbuf.at[chunk, slots],
+            dst_ref=rbuf.at[chunk, slots],
+            send_sem=rsend,
+            recv_sem=rrecv.at[chunk, source],
+            device_id={"col": mirror},
+            device_id_type=MESH,
+        )
+
+    def lcopy(slot, to):
         return pltpu.make_async_remote_copy(
             src_ref=lbuf.at[slot],
             dst_ref=lbuf.at[slot],
-            send_sem=lsend.at[send],
+            send_sem=lsend,
             recv_sem=lrecv.at[slot],
             device_id={"col": to},
             device_id_type=MESH,
         )
 
+    own = pltpu.make_async_copy(sbuf.at[:, me], rbuf.at[:, me], loads.at[0])
+    own.start()
     pl.semaphore_wait(barrier, n - 1)
 
     mates = [base + lax.rem(me - base + 2 * j, half) for j in range(1, half // 2)]
@@ -176,12 +195,9 @@
     sends = []
 
     def send_left(slot, to):
-        copy = lcopy(slot, to, len(sends))
+        copy = lcopy(slot, to)
         copy.start()
         sends.append(copy)
-
-    def other(slot):
-        return lax.rem(slot + half, n)
 
     for to in [mirror] + mates + [partner]:
         send_left(me, to)
@@ -202,82 +218,91 @@
         block = jnp.dot(chosen, weight_ref[...], preferred_element_type=jnp.float32)
         wturn[:, start : start + LANES] = block.T.astype(jnp.bfloat16)
 
-    lcopy(mirror, me, 0).wait_recv()
+    lcopy(mirror, me).wait_recv()
     for to in mates + [partner]:
         send_left(mirror, to)
     for chunk in range(1, chunks):
         send_chunk(chunk)
     for source in sources:
         for slot in (source, other(source)):
-            lcopy(slot, me, 0).wait_recv()
+            lcopy(slot, me).wait_recv()
             send_left(slot, partner)
     for j in range(half // 2):
         slot = base + lax.rem(partner - base + 2 * j, half)
         for slot in (slot, other(slot)):
-            lcopy(slot, me, 0).wait_recv()
+            lcopy(slot, me).wait_recv()
     for s in range(0, n, LANES // TILE):
         block = jnp.concatenate([lbuf[s + p] for p in range(LANES // TILE)], axis=0)
         lturn[:, s * TILE : s * TILE + LANES] = block.T
 
-    def place(slot, block):
-        start = pl.multiple_of(slot * TILE, TILE)
-        for e, wide in enumerate(unpack_columns(cols, period, block)):
-            rwide[pl.ds(start, TILE), e * LANES : (e + 1) * LANES] = wide
-
-    def multiply(step, carry):
-        lanes = pl.ds(pl.multiple_of(step * 2 * LANES, 2 * LANES), 2 * LANES)
+    def place(chunk, source):
+        for p in range(span):
+            slot = source * span + p
+            start = pl.multiple_of(slot * TILE, TILE)
+            block = [rbuf[chunk, slot, :, u * LANES : (u + 1) * LANES] for u in range(turns)]
+            for e, wide in enumerate(unpack_columns(cols, period, block)):
+                rwide[pl.ds(start, TILE), e * LANES : (e + 1) * LANES] = wide
+
+    def multiply(step):
+        lanes = slice(step * 2 * LANES, (step + 1) * 2 * LANES)
         product = jnp.dot(
             lturn[...], rwide[:, lanes], preferred_element_type=jnp.float32
         ).astype(jnp.bfloat16)
         for side_e in range(2):
-            at = pl.ds(pl.multiple_of((step * 2 + side_e) * width, width), width)
+            at = (step * 2 + side_e) * width
             for i in range(rows):
                 side = (i % 2) * LANES
-                flat[i // 2, at, side : side + LANES] = product[
+                flat[i // 2, at : at + width, side : side + LANES] = product[
                     i * width : (i + 1) * width, side_e * LANES : (side_e + 1) * LANES
                 ]
-        return carry
-
+
+    def project(chunk, step):
+        update = jnp.dot(
+            wturn[:, chunk * deep : (chunk + 1) * deep], flat[step],
+            preferred_element_type=jnp.float32,
+        )
+        if chunk:
+            update = update + partial[step]
+        if chunk < chunks - 1:
+            partial[step] = update
+            return
+        update = update.T * (1.0 / seqs) + bias_ref[...]
+        update = update.astype(out_ref.dtype)
+        out_ref[2 * step] = update[:cols]
+        out_ref[2 * step + 1] = update[LANES : LANES + cols]
+
+    low = layer < LAYERS // 2
+    sibling = layer + 1 - 2 * lax.rem(layer, 2)
+    outer = jnp.where(low, LAYERS - 1, 0)
+    inner = jnp.where(low, LAYERS // 2, LAYERS // 2 - 1)
+    own.wait()
     for chunk in range(chunks):
-        place(me, [sbuf[chunk, me, :, u * LANES : (u + 1) * LANES] for u in range(turns)])
-
-        def arrive(k, carry, chunk=chunk):
-            slot = lax.rem(me + n - k, n)
-            rcopy(chunk, slot, slot).wait_recv()
-            place(slot, [rbuf[chunk, slot, :, u * LANES : (u + 1) * LANES] for u in range(turns)])
-            return carry
-
-        lax.fori_loop(1, n, arrive, 0)
-        lax.fori_loop(0, period // 2, multiply, 0)
-
-        def project(pair, carry, chunk=chunk):
-            for step in (2 * pair, 2 * pair + 1):
-                update = jnp.dot(
-                    wturn[:, chunk * deep : (chunk + 1) * deep], flat[step],
-                    preferred_element_type=jnp.float32,
-                )
-                if chunk:
-                    update = update + partial[step]
-                if chunk < chunks - 1:
-                    partial[step] = update
-                else:
-                    update = update.T * (1.0 / seqs) + bias_ref[...]
-                    update = update.astype(out_ref.dtype)
-                    out_ref[2 * step] = update[:cols]
-                    out_ref[2 * step + 1] = update[LANES : LANES + cols]
-            return carry
-
-        lax.fori_loop(0, rows // 4, project, 0)
-
-    for chunk in range(chunks):
-
-        def sent(k, carry, chunk=chunk):
-            rcopy(chunk, lax.rem(me + k, n), me).wait_send()
-            return carry
-
-        lax.fori_loop(1, n, sent, 0)
-    for copy in sends:
-        copy.wait_send()
+        arrival(chunk, layer, span - 1).wait_recv()
+        place(chunk, layer)
+        for source in (sibling, outer, inner):
+            arrival(chunk, source, span).wait_recv()
+            place(chunk, source)
+        for step in range(period // 2):
+            multiply(step)
+        for step in range(rows // 2):
+            project(chunk, step)
+
+    pltpu.make_async_remote_copy(
+        src_ref=sbuf.at[:, pl.ds(0, n - 1)],
+        dst_ref=rbuf.at[:, pl.ds(0, n - 1)],
+        send_sem=rsend,
+        recv_sem=rrecv.at[0, 0],
+        device_id={"col": mirror},
+        device_id_type=MESH,
+    ).wait_send()
+    pltpu.make_async_remote_copy(
+        src_ref=lbuf.at[pl.ds(0, len(sends))],
+        dst_ref=lbuf.at[pl.ds(0, len(sends))],
+        send_sem=lsend,
+        recv_sem=lrecv.at[0],
+        device_id={"col": mirror},
+        device_id_type=MESH,
+    ).wait_send()
 
 
 def packed_call(n, left, right, out_weight, out_bias):
@@ -312,13 +337,13 @@
             pltpu.VMEM((pair, width * width), bf16),
             pltpu.VMEM((rows // 2, period * width, 2 * LANES), bf16),
             pltpu.VMEM((rows // 2, pair, 2 * LANES), f32),
-            dma((chunks, n)), dma((chunks, n)), dma((n,)), dma((n,)),
+            dma(()), dma((chunks, LAYERS)), dma(()), dma((n,)),
             dma((3 + width // TILE,)),
         ],
         compiler_params=pltpu.CompilerParams(
-            collective_id=0, has_side_effects=True, vmem_limit_bytes=60 * 1024 * 1024
+            collective_id=0, has_side_effects=True, vmem_limit_bytes=40 * 1024 * 1024
         ),
-    )(left, jnp.transpose(right, (0, 2, 1)), out_weight, out_bias.reshape(1, pair))
+    )(*(pltpu.with_memory_space_constraint(x, pltpu.HBM) for x in (left, jnp.transpose(right, (0, 2, 1)), out_weight, out_bias.reshape(1, pair))))
 
 
 def packs(n, left, right):
@@ -573,7 +598,7 @@
             dma((n // GROUP,)), dma((n,)), dma((n // GROUP, GROUP)), dma((chunks + 1,)),
         ],
         compiler_params=pltpu.CompilerParams(
-            collective_id=0, has_side_effects=True, vmem_limit_bytes=60 * 1024 * 1024
+            collective_id=0, has_side_effects=True, vmem_limit_bytes=40 * 1024 * 1024
         ),
     )(jnp.transpose(right, (0, 2, 1)), left.reshape(local, rows * width), out_weight, out_bias.reshape(1, pair))
 

time: 45.2 us -> 38.5 us (0.85)
  the two profiles are of different devices: /device:TPU:10 before, /device:TPU:0 now
where the time goes in v3:
time: 38.5 us; the launch traced here: 38.4 us
  Pallas kernels  37.5 us (97%)
  local copies, waits for them, and re-layouts  0.84 us (2%)
    pallas_call x1, Pallas kernels, packed_call(): pl.pallas_call(functools.partial(packed_kernel, n, cols, period), out_sha...  37.5 us
    unnamed x1, local copies, waits for them, and re-layouts  0.84 us

profile of v3, /device:TPU:0, one launch (start us, length us, event | category | flops | bytes accessed | tf_op | source)
XLA Modules:
  0.0 38.4 jit_solution(10913146132261612704)
XLA Ops:
  0.0 37.5 %shard_map.46 = bf16[32,80,128]{2,1,0:T(8,128)(2,1)S(1)} custom-call(bf16[16,32,32]{2,1,0:T(8,128)(2,1)} %left_hbm.1, bf16[16,32,1280]{2,1,0:T(8,128)(2,1)} %bitcast.2, bf16[1024,128]{1,0:T(8,128)(2,1)} %weight_hbm.1, f32[1,128]{1,0:T(1,128)} %bitcast.3), custom_call_target="tpu_custom_call" | custom-call | tf_op jit(solution)/shard_map/pallas_call | solution.py:320
  37.6 0.8 %copy.6 = bf16[32,80,128]{2,1,0:T(8,128)(2,1)} copy(bf16[32,80,128]{2,1,0:T(8,128)(2,1)S(1)} %shard_map.46) | data formatting | bytes 1310720

commit v4 on v3

--- a/solution.py
+++ b/solution.py
@@ -67,15 +67,20 @@
 
 def packed_kernel(
     n, cols, period, left_hbm, right_hbm, weight_hbm, bias_hbm, out_ref,
-    left_ref, right_ref, weight_ref, bias_ref, lspread, rspread, sbuf, rbuf, lbuf,
+    left_ref, right_ref, weight_ref, bias_ref, bias_turned, lspread, rspread, sbuf, rbuf, lbuf,
     rwide, lturn, wturn, flat, partial,
-    rsend, rrecv, lsend, lrecv, loads,
+    rsend, rrecv, lsend, lrecv, loads, edges_in, layer_in, far_in, all_in,
 ):
     me = lax.axis_index("col")
-    half, span = n // 2, n // LAYERS
-    base = me // half * half
-    layer = me // span
+    span = n // LAYERS
+    layer, place_in = me // span, lax.rem(me, span)
+    sibling = layer + 1 - 2 * lax.rem(layer, 2)
+    low = layer < LAYERS // 2
+    is_inner = (layer == LAYERS // 2 - 1) | (layer == LAYERS // 2)
+    outer = jnp.where(low, LAYERS - 1, 0)
+    inner = jnp.where(low, LAYERS // 2, LAYERS // 2 - 1)
     partner = me + 1 - 2 * lax.rem(me, 2)
+    near = sibling * span + place_in
 
     def other(slot):
         return (LAYERS - 1 - slot // span) * span + lax.rem(slot, span)
@@ -88,12 +93,20 @@
     per_half = chunks // halves
     channels = width * width
     deep = period * width
+    groups = [(0, per_half)] + [(chunk, 1) for chunk in range(per_half, chunks)]
 
     barrier = pltpu.get_barrier_semaphore()
-    for k in range(1, n):
-        pl.semaphore_signal(
-            barrier, inc=1, device_id={"col": lax.rem(me + k, n)}, device_id_type=MESH
-        )
+
+    def greet(semaphore, to):
+        pl.semaphore_signal(semaphore, inc=1, device_id={"col": to}, device_id_type=MESH)
+
+    @pl.when(is_inner)
+    def _():
+        for p in range(span):
+            greet(barrier, inner * span + p)
+        for p in range(span):
+            greet(barrier, sibling * span + p)
+
     fetch_left = pltpu.make_async_copy(left_hbm, left_ref, loads.at[0])
     fetch_weight = pltpu.make_async_copy(weight_hbm, weight_ref, loads.at[1])
     fetch_bias = pltpu.make_async_copy(bias_hbm, bias_ref, loads.at[2])
@@ -105,27 +118,16 @@
         )
         for h in range(halves)
     ]
-    fetch_left.start()
     for fetch in fetch_right:
         fetch.start()
+    fetch_left.start()
     fetch_weight.start()
     fetch_bias.start()
 
-    fetch_left.wait()
-    for s in range(local):
-        lspread[s * rows : (s + 1) * rows, :width] = left_ref[s].astype(jnp.float32)
-    lane = lane_index()
-    join = LANES // width
-    for t in range(rows // join):
-        block = lspread[pl.ds(t * join, local, stride=rows), :]
-        for k in range(1, join):
-            piece = lspread[pl.ds(t * join + k, local, stride=rows), :]
-            block = pick(lane, k * width, block, turn_lanes(piece, k * width))
-        lbuf[me, :, t * LANES : (t + 1) * LANES] = block.astype(jnp.bfloat16)
-
     turns = cols * period // LANES
     cycles = n // period
-    for h in range(halves):
+
+    def spread_half(h):
         fetch_right[h].wait()
         for s in range(local):
             for t in range(turns * cycles):
@@ -133,8 +135,9 @@
                     s, h * TILE : (h + 1) * TILE, t * LANES : (t + 1) * LANES
                 ].astype(jnp.float32)
 
-        def pack(step, carry, h=h):
-            chunk, cycle = step // cycles, lax.rem(step, cycles)
+    def pack_half(h, first, count):
+        def pack(step, carry):
+            chunk, cycle = step // count, first + lax.rem(step, count)
             tiles = [
                 [
                     rspread[
@@ -153,25 +156,31 @@
                     ] = out
             return carry
 
-        lax.fori_loop(0, per_half * cycles, pack, 0)
-
-    def rcopy(chunk, to, slot):
-        return pltpu.make_async_remote_copy(
-            src_ref=sbuf.at[chunk, to],
-            dst_ref=rbuf.at[chunk, slot],
+        lax.fori_loop(0, per_half * count, pack, 0)
+
+    def send_right(group, to):
+        first, count = groups[group]
+        pltpu.make_async_remote_copy(
+            src_ref=sbuf.at[pl.ds(first, count), to],
+            dst_ref=rbuf.at[pl.ds(first, count), me],
             send_sem=rsend,
-            recv_sem=rrecv.at[chunk, slot // span],
+            recv_sem=rrecv.at[group, layer],
             device_id={"col": to},
             device_id_type=MESH,
-        )
-
-    def arrival(chunk, source, count):
-        slots = pl.ds(source * span, count)
+        ).start()
+
+    def send_layer(group, target, own=False):
+        for p in range(int(own), span):
+            send_right(group, target * span + lax.rem(place_in + p, span))
+
+    def arrival(group, source, number):
+        first, count = groups[group]
+        slots = pl.ds(source * span, number)
         return pltpu.make_async_remote_copy(
-            src_ref=sbuf.at[chunk, slots],
-            dst_ref=rbuf.at[chunk, slots],
+            src_ref=sbuf.at[pl.ds(first, count), slots],
+            dst_ref=rbuf.at[pl.ds(first, count), slots],
             send_sem=rsend,
-            recv_sem=rrecv.at[chunk, source],
+            recv_sem=rrecv.at[group, source],
             device_id={"col": mirror},
             device_id_type=MESH,
         )
@@ -186,50 +195,115 @@
             device_id_type=MESH,
         )
 
+    mates_near = [
+        sibling * span + lax.rem(place_in + 2 * j, span) for j in range(span // 2)
+    ]
+    mates_own = [
+        layer * span + lax.rem(place_in + 2 * j, span) for j in range(1, span // 2)
+    ]
+    mates = mates_near + mates_own
+
+    half_cycles = cycles // 2
+    mine = jnp.where(low, 0, half_cycles)
+    theirs = half_cycles - mine
+    early = jnp.where(is_inner, theirs, mine)
+    spread_half(0)
+    pack_half(0, early, half_cycles)
+    pl.semaphore_wait(barrier, span)
+
+    @pl.when(is_inner)
+    def _():
+        greet(layer_in, mirror)
+        send_layer(0, inner)
+
+    @pl.when(jnp.logical_not(is_inner))
+    def _():
+        for p in range(span):
+            greet(edges_in, sibling * span + p)
+        send_layer(0, sibling)
+
+    pack_half(0, half_cycles - early, half_cycles)
+    fetch_left.wait()
+    for s in range(local):
+        lspread[s * rows : (s + 1) * rows, :width] = left_ref[s].astype(jnp.float32)
+    lane = lane_index()
+    join = LANES // width
+    for t in range(rows // join):
+        block = lspread[pl.ds(t * join, local, stride=rows), :]
+        for k in range(1, join):
+            piece = lspread[pl.ds(t * join + k, local, stride=rows), :]
+            block = pick(lane, k * width, block, turn_lanes(piece, k * width))
+        lbuf[me, :, t * LANES : (t + 1) * LANES] = block.astype(jnp.bfloat16)
+
+    @pl.when(is_inner)
+    def _():
+        pl.semaphore_wait(edges_in, span)
+        pl.semaphore_wait(layer_in, 1)
+        greet(far_in, mirror)
+        for to in [mirror] + mates + [partner]:
+            lcopy(me, to).start()
+        send_layer(0, layer, own=True)
+        send_layer(0, sibling)
+        pl.semaphore_wait(far_in, 1)
+        greet(all_in, near)
+        send_layer(0, outer)
+
+    @pl.when(jnp.logical_not(is_inner))
+    def _():
+        pl.semaphore_wait(all_in, 1)
+        for to in [mirror] + mates + [partner]:
+            lcopy(me, to).start()
+        send_layer(0, layer, own=True)
+        send_layer(0, inner)
+        send_layer(0, outer)
+
+    for h in range(1, halves):
+        spread_half(h)
+        pack_half(h, 0, cycles)
     own = pltpu.make_async_copy(sbuf.at[:, me], rbuf.at[:, me], loads.at[0])
     own.start()
-    pl.semaphore_wait(barrier, n - 1)
-
-    mates = [base + lax.rem(me - base + 2 * j, half) for j in range(1, half // 2)]
-    sources = [base + lax.rem(me - base + half - 2 * j, half) for j in range(1, half // 2)]
-    sends = []
-
-    def send_left(slot, to):
-        copy = lcopy(slot, to)
-        copy.start()
-        sends.append(copy)
-
-    for to in [mirror] + mates + [partner]:
-        send_left(me, to)
-
-    def send_chunk(chunk):
-        def send_right(k, carry):
-            to = lax.rem(me + k, n)
-            rcopy(chunk, to, me).start()
-            return carry
-
-        lax.fori_loop(1, n, send_right, 0)
-
-    send_chunk(0)
+
+    lcopy(mirror, me).wait_recv()
+    for to in mates + [partner]:
+        lcopy(mirror, to).start()
+
+    later = range(1, len(groups))
+
+    @pl.when(is_inner)
+    def _():
+        for group in later:
+            send_layer(group, outer)
+        for group in later:
+            send_layer(group, sibling)
+            send_layer(group, layer, own=True)
+            send_layer(group, inner)
+
+    @pl.when(jnp.logical_not(is_inner))
+    def _():
+        for group in later:
+            send_layer(group, outer)
+            send_layer(group, inner)
+            send_layer(group, sibling)
+            send_layer(group, layer, own=True)
+
     fetch_weight.wait()
     fetch_bias.wait()
     for start in range(0, channels, LANES):
         chosen = swap_matrix(width, width, start, LANES, channels)
         block = jnp.dot(chosen, weight_ref[...], preferred_element_type=jnp.float32)
         wturn[:, start : start + LANES] = block.T.astype(jnp.bfloat16)
-
-    lcopy(mirror, me).wait_recv()
-    for to in mates + [partner]:
-        send_left(mirror, to)
-    for chunk in range(1, chunks):
-        send_chunk(chunk)
-    for source in sources:
+    pair = bias_ref.shape[1]
+    turned = jnp.broadcast_to(bias_ref[...] * float(seqs), (LANES, pair)).T
+    bias_turned[:, :LANES] = turned
+    bias_turned[:, LANES:] = turned
+
+    for source in mates:
         for slot in (source, other(source)):
             lcopy(slot, me).wait_recv()
-            send_left(slot, partner)
-    for j in range(half // 2):
-        slot = base + lax.rem(partner - base + 2 * j, half)
-        for slot in (slot, other(slot)):
+            lcopy(slot, partner).start()
+    for source in [me] + mates:
+        source = source + 1 - 2 * lax.rem(source, 2)
+        for slot in (source, other(source)):
             lcopy(slot, me).wait_recv()
     for s in range(0, n, LANES // TILE):
         block = jnp.concatenate([lbuf[s + p] for p in range(LANES // TILE)], axis=0)
@@ -261,31 +335,30 @@
             wturn[:, chunk * deep : (chunk + 1) * deep], flat[step],
             preferred_element_type=jnp.float32,
         )
-        if chunk:
-            update = update + partial[step]
+        update = update + (partial[step] if chunk else bias_turned[...])
         if chunk < chunks - 1:
             partial[step] = update
             return
-        update = update.T * (1.0 / seqs) + bias_ref[...]
-        update = update.astype(out_ref.dtype)
-        out_ref[2 * step] = update[:cols]
-        out_ref[2 * step + 1] = update[LANES : LANES + cols]
-
-    low = layer < LAYERS // 2
-    sibling = layer + 1 - 2 * lax.rem(layer, 2)
-    outer = jnp.where(low, LAYERS - 1, 0)
-    inner = jnp.where(low, LAYERS // 2, LAYERS // 2 - 1)
+        update = (update * (1.0 / seqs)).astype(out_ref.dtype)
+        for side in range(2):
+            block = update[:, side * LANES : (side + 1) * LANES].T
+            out_ref[2 * step + side] = block[:cols]
+
     own.wait()
-    for chunk in range(chunks):
-        arrival(chunk, layer, span - 1).wait_recv()
-        place(chunk, layer)
+    for group, (first, count) in enumerate(groups):
+        arrival(group, layer, span - 1).wait_recv()
+        place(first, layer)
         for source in (sibling, outer, inner):
-            arrival(chunk, source, span).wait_recv()
-            place(chunk, source)
-        for step in range(period // 2):
-            multiply(step)
-        for step in range(rows // 2):
-            project(chunk, step)
+            arrival(group, source, span).wait_recv()
+            place(first, source)
+        for chunk in range(first, first + count):
+            if chunk > first:
+                for source in range(LAYERS):
+                    place(chunk, source)
+            for step in range(period // 2):
+                multiply(step)
+            for step in range(rows // 2):
+                project(chunk, step)
 
     pltpu.make_async_remote_copy(
         src_ref=sbuf.at[:, pl.ds(0, n - 1)],
@@ -296,8 +369,8 @@
         device_id_type=MESH,
     ).wait_send()
     pltpu.make_async_remote_copy(
-        src_ref=lbuf.at[pl.ds(0, len(sends))],
-        dst_ref=lbuf.at[pl.ds(0, len(sends))],
+        src_ref=lbuf.at[pl.ds(0, n - 1)],
+        dst_ref=lbuf.at[pl.ds(0, n - 1)],
         send_sem=lsend,
         recv_sem=lrecv.at[0],
         device_id={"col": mirror},
@@ -315,7 +388,7 @@
     lanes = cols * period
     hbm = pl.BlockSpec(memory_space=pltpu.HBM)
     vmem = pl.BlockSpec(memory_space=pltpu.VMEM)
-    dma = pltpu.SemaphoreType.DMA
+    dma, regular = pltpu.SemaphoreType.DMA, pltpu.SemaphoreType.REGULAR
     bf16, f32 = jnp.bfloat16, jnp.float32
     return pl.pallas_call(
         functools.partial(packed_kernel, n, cols, period),
@@ -327,6 +400,7 @@
             pltpu.VMEM((local, width, n * cols), bf16),
             pltpu.VMEM((width * width, pair), bf16),
             pltpu.VMEM((1, pair), f32),
+            pltpu.VMEM((pair, 2 * LANES), f32),
             pltpu.VMEM((local * rows, LANES), f32),
             pltpu.VMEM((n * cols // LANES, local * TILE, LANES), f32),
             pltpu.VMEM((chunks, n, local, lanes), bf16),
@@ -337,8 +411,8 @@
             pltpu.VMEM((pair, width * width), bf16),
             pltpu.VMEM((rows // 2, period * width, 2 * LANES), bf16),
             pltpu.VMEM((rows // 2, pair, 2 * LANES), f32),
-            dma(()), dma((chunks, LAYERS)), dma(()), dma((n,)),
-            dma((3 + width // TILE,)),
+            dma(()), dma((1 + chunks - chunks * TILE // width, LAYERS)), dma(()), dma((n,)),
+            dma((3 + width // TILE,)), regular, regular, regular, regular,
         ],
         compiler_params=pltpu.CompilerParams(
             collective_id=0, has_side_effects=True, vmem_limit_bytes=40 * 1024 * 1024
@@ -354,7 +428,8 @@
         local == TILE and cols <= LANES and rows % 4 == 0 and rows <= 32
         and LANES % width == 0 and rows % (LANES // width) == 0
         and width % TILE == 0 and TILE % period == 0 and period % 2 == 0
-        and n % period == 0 and n % (LANES // TILE) == 0 and n % 4 == 0
+        and n % period == 0 and n % (LANES // TILE) == 0 and n % (2 * LAYERS) == 0
+        and width // period % (width // TILE) == 0 and n // period % 2 == 0
     )
 
 

time: 38.5 us -> 37.3 us (0.969)
  the two profiles are of different devices: /device:TPU:0 before, /device:TPU:10 now
where the time goes in v4:
time: 37.3 us; the launch traced here: 36.7 us
  Pallas kernels  35.9 us (96%)
  local copies, waits for them, and re-layouts  0.84 us (2%)
    pallas_call x1, Pallas kernels, packed_call(): pl.pallas_call(functools.partial(packed_kernel, n, cols, period), out_sha...  35.9 us
    unnamed x1, local copies, waits for them, and re-layouts  0.84 us

profile of v4, /device:TPU:10, one launch (start us, length us, event | category | flops | bytes accessed | tf_op | source)
XLA Modules:
  0.0 36.7 jit_solution(2788614474532281709)
XLA Ops:
  0.0 35.9 %shard_map.46 = bf16[32,80,128]{2,1,0:T(8,128)(2,1)S(1)} custom-call(bf16[16,32,32]{2,1,0:T(8,128)(2,1)} %left_hbm.1, bf16[16,32,1280]{2,1,0:T(8,128)(2,1)} %bitcast.2, bf16[1024,128]{1,0:T(8,128)(2,1)} %weight_hbm.1, f32[1,128]{1,0:T(1,128)} %bitcast.3), custom_call_target="tpu_custom_call" | custom-call | tf_op jit(solution)/shard_map/pallas_call | solution.py:393
  35.9 0.8 %copy.6 = bf16[32,80,128]{2,1,0:T(8,128)(2,1)} copy(bf16[32,80,128]{2,1,0:T(8,128)(2,1)S(1)} %shard_map.46) | data formatting | bytes 1310720

commit v5 on v4

--- a/solution.py
+++ b/solution.py
@@ -94,6 +94,8 @@
     channels = width * width
     deep = period * width
     groups = [(0, per_half)] + [(chunk, 1) for chunk in range(per_half, chunks)]
+    rest = len(groups)
+    groups.append((per_half, chunks - per_half))
 
     barrier = pltpu.get_barrier_semaphore()
 
@@ -267,22 +269,40 @@
     for to in mates + [partner]:
         lcopy(mirror, to).start()
 
-    later = range(1, len(groups))
-
-    @pl.when(is_inner)
+    later = range(1, rest)
+
+    @pl.when(is_inner & low)
     def _():
         for group in later:
+            send_layer(group, inner)
+            send_layer(group, sibling)
+            send_layer(group, layer, own=True)
             send_layer(group, outer)
+
+    def send_part(group, target, part):
+        for p in range(span // 2):
+            turn = lax.rem(place_in + p, span // 2)
+            send_right(group, target * span + part * (span // 2) + turn)
+
+    @pl.when(is_inner & jnp.logical_not(low))
+    def _():
         for group in later:
             send_layer(group, sibling)
             send_layer(group, layer, own=True)
+        for group in later[:-1]:
+            send_layer(group, outer)
+        send_part(later[-1], outer, 0)
+        for group in later[:-1]:
             send_layer(group, inner)
+        send_part(later[-1], outer, 1)
+        send_part(later[-1], inner, 0)
+        send_part(later[-1], inner, 1)
 
     @pl.when(jnp.logical_not(is_inner))
     def _():
+        send_layer(rest, outer)
+        send_layer(rest, inner)
         for group in later:
-            send_layer(group, outer)
-            send_layer(group, inner)
             send_layer(group, sibling)
             send_layer(group, layer, own=True)
 
@@ -345,12 +365,16 @@
             out_ref[2 * step + side] = block[:cols]
 
     own.wait()
-    for group, (first, count) in enumerate(groups):
+    for group, (first, count) in enumerate(groups[:rest]):
         arrival(group, layer, span - 1).wait_recv()
         place(first, layer)
-        for source in (sibling, outer, inner):
-            arrival(group, source, span).wait_recv()
-            place(first, source)
+        arrival(group, sibling, span).wait_recv()
+        place(first, sibling)
+        if group < 2:
+            arrival(rest if group else group, outer, span).wait_recv()
+        place(first, outer)
+        arrival(group, inner, span).wait_recv()
+        place(first, inner)
         for chunk in range(first, first + count):
             if chunk > first:
                 for source in range(LAYERS):
@@ -411,7 +435,7 @@
             pltpu.VMEM((pair, width * width), bf16),
             pltpu.VMEM((rows // 2, period * width, 2 * LANES), bf16),
             pltpu.VMEM((rows // 2, pair, 2 * LANES), f32),
-            dma(()), dma((1 + chunks - chunks * TILE // width, LAYERS)), dma(()), dma((n,)),
+            dma(()), dma((2 + chunks - chunks * TILE // width, LAYERS)), dma(()), dma((n,)),
             dma((3 + width // TILE,)), regular, regular, regular, regular,
         ],
         compiler_params=pltpu.CompilerParams(

time: 37.3 us -> 36.7 us (0.984)
  Pallas kernels: 35.9 us -> 35.2 us
    pallas_call x1, Pallas kernels: 35.9 us -> 35.2 us  [packed_call(): pl.pallas_call(functools.partial(packed_kernel, n, cols, period), out_sha...]
where the time goes in v5:
time: 36.7 us; the launch traced here: 36 us
  Pallas kernels  35.2 us (96%)
  local copies, waits for them, and re-layouts  0.84 us (2%)
    pallas_call x1, Pallas kernels, packed_call(): pl.pallas_call(functools.partial(packed_kernel, n, cols, period), out_sha...  35.2 us
    unnamed x1, local copies, waits for them, and re-layouts  0.84 us

profile of v5, /device:TPU:10, one launch (start us, length us, event | category | flops | bytes accessed | tf_op | source)
XLA Modules:
  0.0 36.0 jit_solution(4411323329391455242)
XLA Ops:
  0.0 35.2 %shard_map.46 = bf16[32,80,128]{2,1,0:T(8,128)(2,1)S(1)} custom-call(bf16[16,32,32]{2,1,0:T(8,128)(2,1)} %left_hbm.1, bf16[16,32,1280]{2,1,0:T(8,128)(2,1)} %bitcast.2, bf16[1024,128]{1,0:T(8,128)(2,1)} %weight_hbm.1, f32[1,128]{1,0:T(1,128)} %bitcast.3), custom_call_target="tpu_custom_call" | custom-call | tf_op jit(solution)/shard_map/pallas_call | solution.py:417
  35.2 0.8 %copy.6 = bf16[32,80,128]{2,1,0:T(8,128)(2,1)} copy(bf16[32,80,128]{2,1,0:T(8,128)(2,1)S(1)} %shard_map.46) | data formatting | bytes 1310720

commit v6 on v5

--- a/solution.py
+++ b/solution.py
@@ -291,20 +291,24 @@
             send_layer(group, layer, own=True)
         for group in later[:-1]:
             send_layer(group, outer)
+        for group in later[:-1]:
+            send_part(group, inner, 0)
         send_part(later[-1], outer, 0)
         for group in later[:-1]:
-            send_layer(group, inner)
+            send_part(group, inner, 1)
+        for p in range(1, span // 2):
+            send_right(later[-1], inner * span + p)
         send_part(later[-1], outer, 1)
-        send_part(later[-1], inner, 0)
+        send_right(later[-1], inner * span)
         send_part(later[-1], inner, 1)
 
     @pl.when(jnp.logical_not(is_inner))
     def _():
-        send_layer(rest, outer)
-        send_layer(rest, inner)
         for group in later:
             send_layer(group, sibling)
             send_layer(group, layer, own=True)
+        send_layer(rest, outer)
+        send_layer(rest, inner)
 
     fetch_weight.wait()
     fetch_bias.wait()

time: 36.7 us -> 36.4 us (level); the launches traced: 36 us -> 36.3 us
  no operation moved by 1% of the time
where the time goes in v6:
time: 36.4 us; the launch traced here: 36.3 us
  Pallas kernels  35.4 us (97%)
  local copies, waits for them, and re-layouts  0.84 us (2%)
    pallas_call x1, Pallas kernels, packed_call(): pl.pallas_call(functools.partial(packed_kernel, n, cols, period), out_sha...  35.4 us
    unnamed x1, local copies, waits for them, and re-layouts  0.84 us

profile of v6, /device:TPU:10, one launch (start us, length us, event | category | flops | bytes accessed | tf_op | source)
XLA Modules:
  0.0 36.3 jit_solution(1483113986264247147)
XLA Ops:
  0.0 35.4 %shard_map.46 = bf16[32,80,128]{2,1,0:T(8,128)(2,1)S(1)} custom-call(bf16[16,32,32]{2,1,0:T(8,128)(2,1)} %left_hbm.1, bf16[16,32,1280]{2,1,0:T(8,128)(2,1)} %bitcast.2, bf16[1024,128]{1,0:T(8,128)(2,1)} %weight_hbm.1, f32[1,128]{1,0:T(1,128)} %bitcast.3), custom_call_target="tpu_custom_call" | custom-call | tf_op jit(solution)/shard_map/pallas_call | solution.py:421
  35.4 0.8 %copy.6 = bf16[32,80,128]{2,1,0:T(8,128)(2,1)} copy(bf16[32,80,128]{2,1,0:T(8,128)(2,1)S(1)} %shard_map.46) | data formatting | bytes 1310720

commit v7 on v6

--- a/solution.py
+++ b/solution.py
@@ -13,6 +13,7 @@
 TILE = 16
 GROUP = 4
 LAYERS = 4
+STORES = 8
 
 
 def lane_index():
@@ -66,9 +67,9 @@
 
 
 def packed_kernel(
-    n, cols, period, left_hbm, right_hbm, weight_hbm, bias_hbm, out_ref,
+    n, cols, period, left_hbm, right_hbm, weight_hbm, bias_hbm, flat, partial, last,
     left_ref, right_ref, weight_ref, bias_ref, bias_turned, lspread, rspread, sbuf, rbuf, lbuf,
-    rwide, lturn, wturn, flat, partial,
+    rwide, lturn, wturn,
     rsend, rrecv, lsend, lrecv, loads, edges_in, layer_in, far_in, all_in,
 ):
     me = lax.axis_index("col")
@@ -316,6 +317,7 @@
         chosen = swap_matrix(width, width, start, LANES, channels)
         block = jnp.dot(chosen, weight_ref[...], preferred_element_type=jnp.float32)
         wturn[:, start : start + LANES] = block.T.astype(jnp.bfloat16)
+    last[...] = wturn[:, channels - deep :]
     pair = bias_ref.shape[1]
     turned = jnp.broadcast_to(bias_ref[...] * float(seqs), (LANES, pair)).T
     bias_turned[:, :LANES] = turned
@@ -359,14 +361,7 @@
             wturn[:, chunk * deep : (chunk + 1) * deep], flat[step],
             preferred_element_type=jnp.float32,
         )
-        update = update + (partial[step] if chunk else bias_turned[...])
-        if chunk < chunks - 1:
-            partial[step] = update
-            return
-        update = (update * (1.0 / seqs)).astype(out_ref.dtype)
-        for side in range(2):
-            block = update[:, side * LANES : (side + 1) * LANES].T
-            out_ref[2 * step + side] = block[:cols]
+        partial[step] = update + (partial[step] if chunk else bias_turned[...])
 
     own.wait()
     for group, (first, count) in enumerate(groups[:rest]):
@@ -385,8 +380,9 @@
                     place(chunk, source)
             for step in range(period // 2):
                 multiply(step)
-            for step in range(rows // 2):
-                project(chunk, step)
+            if chunk < chunks - 1:
+                for step in range(rows // 2):
+                    project(chunk, step)
 
     pltpu.make_async_remote_copy(
         src_ref=sbuf.at[:, pl.ds(0, n - 1)],
@@ -406,6 +402,24 @@
     ).wait_send()
 
 
+def finish_kernel(seqs, cols, flat, partial, last, out_hbm, out_ref, sems):
+    steps = flat.shape[0]
+    per = steps // STORES
+    copies = []
+    for store in range(STORES):
+        for step in range(store * per, (store + 1) * per):
+            update = jnp.dot(last[...], flat[step], preferred_element_type=jnp.float32)
+            update = ((update + partial[step]) * (1.0 / seqs)).astype(out_ref.dtype)
+            for side in range(2):
+                block = update[:, side * LANES : (side + 1) * LANES].T
+                out_ref[2 * step + side] = block[:cols]
+        at = pl.ds(2 * store * per, 2 * per)
+        copies.append(pltpu.make_async_copy(out_ref.at[at], out_hbm.at[at], sems.at[store]))
+        copies[-1].start()
+    for copy in copies:
+        copy.wait()
+
+
 def packed_call(n, left, right, out_weight, out_bias):
     local, rows, width = left.shape
     cols = right.shape[1] // n
@@ -418,11 +432,15 @@
     vmem = pl.BlockSpec(memory_space=pltpu.VMEM)
     dma, regular = pltpu.SemaphoreType.DMA, pltpu.SemaphoreType.REGULAR
     bf16, f32 = jnp.bfloat16, jnp.float32
-    return pl.pallas_call(
+    parts = pl.pallas_call(
         functools.partial(packed_kernel, n, cols, period),
-        out_shape=jax.ShapeDtypeStruct((rows, cols, pair), bf16),
+        out_shape=(
+            jax.ShapeDtypeStruct((rows // 2, period * width, 2 * LANES), bf16),
+            jax.ShapeDtypeStruct((rows // 2, pair, 2 * LANES), f32),
+            jax.ShapeDtypeStruct((pair, period * width), bf16),
+        ),
         in_specs=[hbm] * 4,
-        out_specs=vmem,
+        out_specs=(vmem,) * 3,
         scratch_shapes=[
             pltpu.VMEM((local, rows, width), bf16),
             pltpu.VMEM((local, width, n * cols), bf16),
@@ -437,8 +455,6 @@
             pltpu.VMEM((seqs, period * LANES), bf16),
             pltpu.VMEM((rows * width, seqs), bf16),
             pltpu.VMEM((pair, width * width), bf16),
-            pltpu.VMEM((rows // 2, period * width, 2 * LANES), bf16),
-            pltpu.VMEM((rows // 2, pair, 2 * LANES), f32),
             dma(()), dma((2 + chunks - chunks * TILE // width, LAYERS)), dma(()), dma((n,)),
             dma((3 + width // TILE,)), regular, regular, regular, regular,
         ],
@@ -446,6 +462,14 @@
             collective_id=0, has_side_effects=True, vmem_limit_bytes=40 * 1024 * 1024
         ),
     )(*(pltpu.with_memory_space_constraint(x, pltpu.HBM) for x in (left, jnp.transpose(right, (0, 2, 1)), out_weight, out_bias.reshape(1, pair))))
+    return pl.pallas_call(
+        functools.partial(finish_kernel, seqs, cols),
+        out_shape=jax.ShapeDtypeStruct((rows, cols, pair), bf16),
+        in_specs=[vmem] * 3,
+        out_specs=hbm,
+        scratch_shapes=[pltpu.VMEM((rows, cols, pair), bf16), dma((STORES,))],
+        compiler_params=pltpu.CompilerParams(vmem_limit_bytes=16 * 1024 * 1024),
+    )(*(pltpu.with_memory_space_constraint(x, pltpu.VMEM) for x in parts))
 
 
 def packs(n, left, right):
@@ -453,7 +477,7 @@
     cols = right.shape[1] // n
     period = LANES // math.gcd(cols, LANES)
     return (
-        local == TILE and cols <= LANES and rows % 4 == 0 and rows <= 32
+        local == TILE and cols <= LANES and rows % (2 * STORES) == 0 and rows <= 32
         and LANES % width == 0 and rows % (LANES // width) == 0
         and width % TILE == 0 and TILE % period == 0 and period % 2 == 0
         and n % period == 0 and n % (LANES // TILE) == 0 and n % (2 * LAYERS) == 0

time: 36.4 us -> 36.4 us (level)
  Pallas kernels: 35.4 us -> 36.3 us
  local copies, waits for them, and re-layouts: 0.84 us -> 0 us
    pallas_call x0 -> x1, Pallas kernels: none -> 1.22 us  [packed_call(): pl.pallas_call(functools.partial(finish_kernel, seqs, cols), out_shape=ja...]
    unnamed x1 -> x0, local copies, waits for them, and re-layouts: 0.84 us -> none
    pallas_call x1, Pallas kernels: 35.4 us -> 35 us  [packed_call(): pl.pallas_call(functools.partial(packed_kernel, n, cols, period), out_sha...]
where the time goes in v7:
time: 36.4 us; the launch traced here: 36.3 us
  Pallas kernels  36.3 us (100%)
    pallas_call x1, Pallas kernels, packed_call(): pl.pallas_call(functools.partial(packed_kernel, n, cols, period), out_sha...  35 us
    pallas_call x1, Pallas kernels, packed_call(): pl.pallas_call(functools.partial(finish_kernel, seqs, cols), out_shape=ja...  1.22 us

profile of v7, /device:TPU:10, one launch (start us, length us, event | category | flops | bytes accessed | tf_op | source)
XLA Modules:
  0.0 36.3 jit_solution(4331525129968817975)
XLA Ops:
  0.0 35.0 %shard_map.46 = (bf16[16,256,256]{2,1,0:T(8,128)(2,1)S(1)}, f32[16,128,256]{2,1,0:T(8,128)S(1)}, bf16[128,256]{1,0:T(8,128)(2,1)S(1)}) custom-call(bf16[16,32,32]{2,1,0:T(8,128)(2,1)} %left_hbm.1, bf16[16,32,1280]{2,1,0:T(8,128)(2,1)} %bitcast.2, bf16[1024,128]{1,0:T(8,128)(2,1)} %weight_hbm.1, f32[1,128]{1,0:T(1,128)} %bitcast.3), custom_call_target="tpu_custom_call" | custom-call | tf_op jit(solution)/shard_map/pallas_call | solution.py:435
  35.0 1.2 %shard_map.47 = bf16[32,80,128]{2,1,0:T(8,128)(2,1)} custom-call(bf16[16,256,256]{2,1,0:T(8,128)(2,1)S(1)} %get-tuple-element.8.flat, f32[16,128,256]{2,1,0:T(8,128)S(1)} %get-tuple-element.9.partial, bf16[128,256]{1,0:T(8,128)(2,1)S(1)} %get-tuple-element.10.last), custom_call_target="tpu_custom_call" | custom-call | tf_op jit(solution)/shard_map/pallas_call | solution.py:465
